TPU v7x, 32 devices: a whole 2x2x4 slice. The times are simulated.
32 devices in a mesh: dep: 4 (over z), col: 2 (over y), row: 4 (over x, core).
Axes of the slice: x: 2, y: 2, z: 4, core: 2. Of those that a mesh axis runs over, the one named last changes fastest.
Arguments:
- a_mat: bfloat16 [5120, 5120], P('row', 'col')
- b_mat: bfloat16 [5120, 5120], P('row', 'col')
Outputs:
- output: float32 [5120, 5120], P('row', ('col', 'dep'))
All inputs are finite; a program needn't handle non-finite values.
Results may differ from a plain program's by a relative error of at most 0.001.
Values are sent between devices in bfloat16 or wider.
A program may use at most 1 GiB of HBM per device.

v0:
```python
import jax
import jax.numpy as jnp
from jax import lax
from jax.sharding import PartitionSpec as P


def solution(mesh):
    n_dep = mesh.shape['dep']
    n_row = mesh.shape['row']
    n_col = mesh.shape['col']

    def local_product(a_blk, b_blk):
        layer_idx = lax.axis_index('dep')
        rows_a, cols_a = a_blk.shape
        cols_b = b_blk.shape[1]
        unit_len = cols_a // (n_row * n_dep)
        a_part = a_blk.reshape(rows_a, n_row, n_dep, unit_len)
        a_part = lax.dynamic_index_in_dim(a_part, layer_idx, axis=2, keepdims=False)
        a_part = a_part.reshape(rows_a, n_row * unit_len)
        b_part = b_blk.reshape(n_col, n_dep, unit_len, cols_b)
        b_part = lax.dynamic_index_in_dim(b_part, layer_idx, axis=1, keepdims=False)
        b_part = b_part.reshape(n_col * unit_len, cols_b)
        a_panel = lax.all_gather(a_part, 'col', axis=1, tiled=True)
        b_panel = lax.all_gather(b_part, 'row', axis=0, tiled=True)
        part_sum = jnp.dot(a_panel, b_panel, preferred_element_type=jnp.float32)
        return lax.psum_scatter(part_sum, 'dep', scatter_dimension=1, tiled=True)

    return jax.shard_map(local_product, mesh=mesh, in_specs=(P('row', 'col'), P('row', 'col')), out_specs=P('row', ('col', 'dep')), check_vma=False)
```

profile of v0, /device:TPU:0, one launch (start us, length us, event | category | flops | bytes accessed | tf_op | source)
XLA Modules:
  0.0 359.1 jit_solution(13049964867029346539)
XLA Ops:
  6.5 0.0 all-gather.3.cloned.1.call-start
  6.5 9.5 %copy.3 = bf16[1280,2560]{0,1:T(8,128)(2,1)} copy(bf16[1280,2560]{1,0:T(8,128)(2,1)} %param.2) | data formatting | bytes 13107200 | tf_op args[0]
  16.0 2.7 constant_dynamic-slice_fusion.1
  18.7 0.0 all-gather.3.cloned.1.call-update
  18.8 0.0 all-gather.5.cloned.1.call-start
  18.8 2.7 constant_dynamic-slice_fusion
  21.5 0.0 all-gather.5.cloned.1.call-update
  21.6 0.0 reduce-scatter.2.cloned.1.call-start
  21.6 46.5 %all-gather.3.cloned.1.call-done = bf16[1280,1280]{0,1:T(8,128)(2,1)} async-done(((bf16[1280,640]{0,1:T(8,128)(2,1)}), bf16[1280,1280]{0,1:T(8,128)(2,1)}) %all-gather.3.cloned.1.call-update) | async-done | bytes 3276816 | tf_op jit(solution)/shard_map/all_gather | solution.py:23
  68.1 49.5 %all-gather.5.cloned.1.call-done = bf16[1280,2560]{1,0:T(8,128)(2,1)} async-done(((bf16[320,2560]{1,0:T(8,128)(2,1)}), bf16[1280,2560]{1,0:T(8,128)(2,1)}) %all-gather.5.cloned.1.call-update) | async-done | bytes 6553616 | tf_op jit(solution)/shard_map/all_gather | solution.py:24
  117.6 14.7 %fusion = f32[1280,2560]{1,0:T(8,128)} fusion(bf16[1280,1280]{0,1:T(8,128)(2,1)} %all-gather.3.cloned.1.call-done, bf16[1280,2560]{1,0:T(8,128)(2,1)} %all-gather.5.cloned.1.call-done), kind=kOutput, calls=%fused_computation.2 | convolution fusion | flops 8388608000 | bytes 22937600 | tf_op jit(solution)/shard_map/dot_general | solution.py:25
  132.3 0.0 reduce-scatter.2.cloned.1.call-update
  132.3 220.3 %reduce-scatter.2.cloned.1.call-done = f32[1280,640]{1,0:T(8,128)} async-done(((f32[1280,2560]{1,0:T(8,128)}), f32[1280,640]{1,0:T(8,128)}) %reduce-scatter.2.cloned.1.call-update) | async-done | bytes 3276816 | tf_op jit(solution)/shard_map/reduce_scatter | solution.py:26
Async XLA Ops:
  6.5 61.6 %all-gather.3.cloned.1.call-start = ((), (), s32[]{:S(2)}) async-start(), calls=%async_computation.1 | async-start | bytes 4915200 | tf_op jit(solution)/shard_map/all_gather | solution.py:23
  18.8 98.9 %all-gather.5.cloned.1.call-start = ((), (), s32[]{:S(2)}) async-start(), calls=%async_computation.2 | async-start | bytes 8192000 | tf_op jit(solution)/shard_map/all_gather | solution.py:24
  21.6 331.0 %reduce-scatter.2.cloned.1.call-start = ((), (), s32[]{:S(2)}) async-start(), calls=%async_computation.3 | async-start | bytes 16384000 | tf_op jit(solution)/shard_map/reduce_scatter | solution.py:26
Sparse Core Ops, SparseCore 0:
  18.9 49.1 all-gather.2
  69.7 47.8 all-gather.4
  132.4 220.0 reduce-scatter.1
where the time goes:
time: 359 us
  waiting for transfers between devices  316 us (88%)
  local copies, waits for them, and re-layouts  14.9 us (4%)
  matrix products  14.7 us (4%)
  between operations  13.1 us (4%)
    reduce_scatter x1, waiting for transfers between devices, local_product(): return lax.psum_scatter(part_sum, 'dep', scatter_dimension=1, tiled=True)  220 us
    all_gather x1, waiting for transfers between devices, local_product(): b_panel = lax.all_gather(b_part, 'row', axis=0, tiled=True)  49.5 us
    all_gather x1, waiting for transfers between devices, local_product(): a_panel = lax.all_gather(a_part, 'col', axis=1, tiled=True)  46.5 us
    dot_general x1, matrix products, local_product(): part_sum = jnp.dot(a_panel, b_panel, preferred_element_type=jnp.float32)  14.7 us
    unnamed x1, local copies, waits for them, and re-layouts  9.5 us
  transfers between devices with their start and end apart: 3, of which 3 were waited for; matrix products, arithmetic and copies ran while one was open for 1% of the time, Pallas kernels for 0%

commit v1 on v0

v1 whole, which is shorter than its diff:
```python
import functools

import jax
import jax.numpy as jnp
from jax import lax
from jax.experimental import pallas as pl
from jax.experimental.pallas import tpu as pltpu
from jax.sharding import PartitionSpec as P

MESH = pl.DeviceIdType.MESH

NY = 16
N_A = 8
N_E = 6
NK = 10
NB = 5
K_A = 5
K_P = 7
N_P = 18
K_R = 11
LAG = 2


def kernel(a_ref, b_ref, o_ref, am, bm, pm, ys, yr, zs, zr, as_, ar, bs, br, es, er, ps, pr, xs, xr, ds_, dr, fs, fr, ls, lr, loc):
    z, y, row = lax.axis_index("dep"), lax.axis_index("col"), lax.axis_index("row")
    x, c = row // 2, row % 2
    rows, depth = a_ref.shape
    quarter = b_ref.shape[0]
    width = o_ref.shape[1]
    ch = rows // 40
    blk = 4 * ch
    kc = quarter // NK
    side = z // 2
    mid = (z == 1) | (z == 2)
    end = jnp.logical_not(mid)
    eq = x == y
    neq = jnp.logical_not(eq)
    mine = (8 + 16 * side) * ch
    oth = (24 - 16 * side) * ch
    end_slice = 3 * side
    to_y = (z, 1 - y, row)
    to_x = (z, y, (1 - x) * 2 + c)
    to_core = (z, y, x * 2 + 1 - c)
    to_pair = (z + 1 - 2 * (z % 2), y, row)
    to_mid = (3 - z, y, row)

    def span(start, n):
        return pl.ds(pl.multiple_of(start, n), n)

    def within(i, n):
        return jnp.clip(i, 0, n - 1)

    def remote(src, dst, send, recv, dev):
        return pltpu.make_async_remote_copy(src_ref=src, dst_ref=dst, send_sem=send, recv_sem=recv, device_id=dev, device_id_type=MESH)

    def copy_y(k):
        k = within(k, NY)
        r = jnp.where(mid, mine + ch * k, jnp.where(k < N_A, ch * k, oth + ch * k))
        return remote(a_ref.at[span(r, ch)], am.at[1, span(r, ch)], ys.at[k], yr.at[k], to_y)

    def pass_rows(r, send, recv, dev):
        return remote(am.at[1, span(r, ch)], am.at[1, span(r, ch)], send, recv, dev)

    def copy_zm(k):
        k = within(k, NY)
        return pass_rows(mine + ch * k, zs.at[k], zr.at[k], to_mid)

    def copy_ze(k):
        k = within(k, N_E)
        return pass_rows(mine + ch * k, es.at[k], er.at[k], to_pair)

    def copy_za(k):
        k = within(k, N_A)
        return pass_rows(ch * k, as_.at[k], ar.at[k], to_pair)

    def lane(i):
        return span(c * quarter + kc * i, kc)

    def copy_zb(i):
        i = within(i, NB)
        return remote(bm.at[1, lane(i)], bm.at[2, lane(i)], bs.at[i], br.at[i], to_pair)

    def copy_x(i):
        i = within(i, 2 * NK - NB)
        extra = jnp.where(mid & neq, NK - NB, 0)
        early = i < extra
        piece = within(jnp.where(early, NB + i, i - extra), NK)
        cols = pl.ds(pl.multiple_of(jnp.where(early, end_slice, z) * width, 128), width)
        slot = jnp.where(early, 2, 1)
        return remote(b_ref.at[span(piece * kc, kc), cols], bm.at[slot, lane(piece)], xs.at[i], xr.at[i], to_x)

    def copy_d(i):
        i = within(i, 2 * NK - NB)
        extra = jnp.where(mid & eq, NK - NB, 0)
        early = i < extra
        piece = within(jnp.where(early, NB + i, i - extra), NK)
        ref = bm.at[jnp.where(early, 2, 1), lane(piece)]
        return remote(ref, ref, ds_.at[i], dr.at[i], to_core)

    def copy_f(i):
        i = within(i, NB)
        ref = bm.at[2, lane(i)]
        return remote(ref, ref, fs.at[i], fr.at[i], to_core)

    own_lane = span(c * quarter, quarter)

    def b_cols(s):
        return b_ref.at[:, pl.ds(pl.multiple_of(s * width, 128), width)]

    load_a = pltpu.make_async_copy(a_ref, am.at[0], loc.at[0])
    load_b = pltpu.make_async_copy(b_cols(z), bm.at[0, own_lane], loc.at[1])
    load_e = pltpu.make_async_copy(b_cols(end_slice), bm.at[2, own_lane], loc.at[2])
    give_b = remote(b_cols(z), bm.at[0, own_lane], ls.at[0], lr.at[0], to_core)
    give_e = remote(b_cols(end_slice), bm.at[2, own_lane], ls.at[1], lr.at[1], to_core)

    def sum_row(j):
        k, t = K_P + j // 2, j % 2
        first = jnp.where(k < K_P + 8, oth + ch * (k - K_P), mine + ch * (NY - 1))
        return jnp.where(t == 0, first, mine + ch * (k - 1))

    def copy_p(j):
        j = within(j, N_P)
        ref = pm.at[span(j * ch, ch)]
        return remote(ref, ref, ps.at[j], pr.at[j], to_pair)

    n_send = jnp.where(mid & neq, 2 * NK - NB, NK)
    n_recv = jnp.where(mid & eq, 2 * NK - NB, NK)

    barrier = pltpu.get_barrier_semaphore()
    for dev in (to_y, to_x, to_core, to_pair):
        pl.semaphore_signal(barrier, inc=1, device_id=dev, device_id_type=MESH)

    @pl.when(mid)
    def _():
        pl.semaphore_signal(barrier, inc=1, device_id=to_mid, device_id_type=MESH)

    pl.semaphore_wait(barrier, jnp.where(mid, 5, 4))

    @pl.loop(0, NY)
    def _(k):
        copy_y(k).start()

        @pl.when(k < n_send)
        def _():
            copy_x(k).start()

    load_b.start()
    give_b.start()
    load_a.start()

    @pl.when(mid & neq)
    def _():
        load_e.start()
        give_e.start()

    @pl.loop(0, rows // ch)
    def _(i):
        o_ref[span(i * ch, ch), :] = jnp.zeros((ch, width), jnp.float32)

    def add_product(half, start, slot, n):
        r = pl.ds(pl.multiple_of(jnp.clip(start, 0, rows - n), n if n < blk else ch), n)
        o_ref[r, :] += jnp.dot(am[half, r, :], bm[slot], preferred_element_type=jnp.float32)

    oth_slot = jnp.where(eq, 1, 0)
    own_slot = jnp.where(eq, 0, 1)

    def take_sums(j):
        j = within(j, N_P)
        copy_p(j).wait_recv()
        o_ref[span(sum_row(j), ch), :] += pm[span(j * ch, ch), :]

    @pl.loop(0, NY)
    def _(k):
        copy_y(k).wait_recv()

        @pl.when(mid)
        def _():
            copy_zm(k).start()

        @pl.when(mid & (k < N_E))
        def _():
            copy_ze(k).start()

        @pl.when(k < n_recv)
        def _():
            copy_x(k).wait_recv()
            copy_d(k).start()

        @pl.when(end & eq & (k < NB))
        def _():
            copy_zb(k).start()

        @pl.when(end & (k >= K_A) & (k < K_A + N_A))
        def _():
            copy_za(k - K_A).start()

        @pl.when(mid & eq & (k >= LAG) & (k < LAG + NB))
        def _():
            copy_zb(k - LAG).wait_recv()
            copy_f(k - LAG).start()

        @pl.when(mid & (k >= LAG))
        def _():
            copy_zm(k - LAG).wait_recv()

        @pl.when(mid & (k >= LAG + K_A) & (k < LAG + K_A + N_A))
        def _():
            copy_za(k - LAG - K_A).wait_recv()

        @pl.when(end & (k >= LAG) & (k < LAG + N_E))
        def _():
            copy_ze(k - LAG).wait_recv()

        @pl.when(k == 1)
        def _():
            load_b.wait()
            give_b.wait_recv()
            load_a.wait()

            @pl.when(mid & neq)
            def _():
                load_e.wait()
                give_e.wait_recv()

        @pl.when(mid & eq & (k == K_P))
        def _():
            @pl.loop(0, NB)
            def _(i):
                copy_d(i).wait_recv()
                copy_f(i).wait_recv()

        @pl.when(mid & (k >= K_P))
        def _():
            @pl.loop(0, 2)
            def _(t):
                j = 2 * (k - K_P) + t
                pm[span(j * ch, ch), :] = jnp.dot(am[1, span(sum_row(j), ch), :], bm[2], preferred_element_type=jnp.float32)
                copy_p(j).start()

        @pl.when((k == K_R) & (end | neq))
        def _():
            @pl.loop(0, NK)
            def _(i):
                copy_d(i).wait_recv()

        own_from = jnp.where(eq, 2, K_R)
        neq_mid_row = jnp.where(k % 4 == 0, mine + blk * (k // 4 - 1), jnp.where(k % 4 == 1, oth + blk * (k // 4 - 1), jnp.where(k == 10, 0, blk)))
        neq_mid_do = (k >= 4) & ((k % 4 < 2) | (k == 10) | (k == 14))
        neq_end_row = jnp.where(k == 4, 0, jnp.where(k == 8, blk, oth + 2 * blk))
        neq_end_do = (k == 4) | (k == 8) | (k == 12)
        eq_end_row = jnp.where(k == K_R, 0, jnp.where(k == K_R + 1, blk, oth + 2 * blk))
        eq_end_do = (k >= K_R) & (k < K_R + 3)
        late_row = jnp.where(mid, neq_mid_row, jnp.where(eq, eq_end_row, neq_end_row))
        late_do = (mid & neq & neq_mid_do) | (end & neq & neq_end_do) | (end & eq & eq_end_do)

        @pl.loop(0, 3)
        def _(t):
            own = t < 2
            do = jnp.where(own, (k >= own_from) & (k < own_from + 5), late_do)

            @pl.when(do)
            def _():
                start = jnp.where(own, blk * (2 * (k - own_from) + t), late_row)
                add_product(jnp.where(own, 0, 1), start, jnp.where(own, own_slot, oth_slot), blk)

        @pl.when(end & (k == jnp.where(eq, 14, 9)))
        def _():
            @pl.loop(0, N_E // 2)
            def _(t):
                add_product(1, mine + 2 * ch * t, oth_slot, 2 * ch)

        @pl.when(end & (k >= K_P + 3))
        def _():
            @pl.loop(0, 2)
            def _(t):
                take_sums(2 * (k - K_P - 3) + t)

    @pl.when(mid)
    def _():
        @pl.loop(NY - LAG, NY - 1)
        def _(k):
            copy_zm(k).wait_recv()

        @pl.when(eq)
        def _():
            @pl.loop(NK - NB, 2 * NK - NB)
            def _(i):
                copy_d(i).wait_recv()

    @pl.loop(0, 10)
    def _(t):
        last = t == 9
        all_row = jnp.where(t < 2, blk * t, jnp.where(t < 6, mine + blk * (t - 2), oth + blk * (t - 6)))
        start = jnp.where(last, oth + 3 * blk, jnp.where(eq, all_row, mine + 3 * blk))

        @pl.when(mid & last)
        def _():
            copy_zm(NY - 1).wait_recv()

        @pl.when(last | (mid & (eq | (t == 0))))
        def _():
            add_product(1, start, oth_slot, blk)

    @pl.when(end)
    def _():
        @pl.loop(2 * (NY - K_P - 3), N_P)
        def _(j):
            take_sums(j)

    @pl.loop(0, NY)
    def _(k):
        copy_y(k).wait_send()

        @pl.when(k < n_send)
        def _():
            copy_x(k).wait_send()

        @pl.when(k < n_recv)
        def _():
            copy_d(k).wait_send()

        @pl.when(mid)
        def _():
            copy_zm(k).wait_send()

        @pl.when(mid & (k < N_E))
        def _():
            copy_ze(k).wait_send()

        @pl.when(end & (k < N_A))
        def _():
            copy_za(k).wait_send()

        @pl.when(end & eq & (k < NB))
        def _():
            copy_zb(k).wait_send()

        @pl.when(mid & eq & (k < NB))
        def _():
            copy_f(k).wait_send()

    give_b.wait_send()

    @pl.when(mid & neq)
    def _():
        give_e.wait_send()

    @pl.when(mid)
    def _():
        @pl.loop(0, N_P)
        def _(j):
            copy_p(j).wait_send()


def solution(mesh):
    def body(a, b):
        rows, depth = a.shape
        quarter, wide = b.shape
        width = wide // mesh.shape["dep"]
        dma = pltpu.SemaphoreType.DMA
        counts = (NY, NY, NY, NY, N_A, N_A, NB, NB, N_E, N_E, N_P, N_P, NY, NY, NY, NY, NB, NB, 2, 2, 3)
        return pl.pallas_call(
            kernel,
            out_shape=jax.ShapeDtypeStruct((rows, width), jnp.float32),
            in_specs=[pl.BlockSpec(memory_space=pl.ANY)] * 2,
            out_specs=pl.BlockSpec(memory_space=pltpu.VMEM),
            scratch_shapes=[
                pltpu.VMEM((2, rows, depth), jnp.bfloat16),
                pltpu.VMEM((3, 2 * quarter, width), jnp.bfloat16),
                pltpu.VMEM((N_P * (rows // 40), width), jnp.float32),
            ]
            + [dma((n,)) for n in counts],
            compiler_params=pltpu.CompilerParams(collective_id=0, has_side_effects=True, vmem_limit_bytes=48 * 2**20),
        )(a, b)

    return jax.shard_map(body, mesh=mesh, in_specs=(P("row", "col"), P("row", "col")), out_specs=P("row", ("col", "dep")), check_vma=False)
```

time: 359 us -> 74.8 us (0.21)
  the two profiles are of different devices: /device:TPU:0 before, /device:TPU:8 now
where the time goes in v1:
time: 74.8 us; the launch traced here: 74.7 us
  Pallas kernels  72.9 us (97%)
  local copies, waits for them, and re-layouts  1.71 us (2%)
    pallas_call x1, Pallas kernels, body(): pl.pallas_call(kernel, out_shape=jax.ShapeDtypeStruct((rows, width), jnp....  72.9 us
    unnamed x1, local copies, waits for them, and re-layouts  1.71 us

profile of v1, /device:TPU:8, one launch (start us, length us, event | category | flops | bytes accessed | tf_op | source)
XLA Modules:
  0.0 74.7 jit_solution(14251549128556039499)
XLA Ops:
  0.0 72.9 %shard_map.28 = f32[1280,640]{1,0:T(8,128)S(1)} custom-call(bf16[1280,2560]{1,0:T(8,128)(2,1)} %a_ref.1, bf16[1280,2560]{1,0:T(8,128)(2,1)} %b_ref.1), custom_call_target="tpu_custom_call" | custom-call | tf_op jit(solution)/shard_map/pallas_call | solution.py:362
  72.9 1.7 %copy.4 = f32[1280,640]{1,0:T(8,128)} copy(f32[1280,640]{1,0:T(8,128)S(1)} %shard_map.28) | data formatting | bytes 6553600

commit v2 on v0

v2 whole, which is shorter than its diff:
```python
import jax
import jax.numpy as jnp
from jax import lax
from jax.experimental import pallas as pl
from jax.experimental.pallas import tpu as pltpu
from jax.sharding import PartitionSpec as P

MESH = pl.DeviceIdType.MESH

PIECES = 40
NY = 16
N_A = 10
N_M = 14
TOP = 30
N_E = 6
NK = 10
NB = 5
K_P = 6
N_P = 18
LAG = 2
PART = 4


def mine(p, n):
    return (p, TOP - p - n)


def oth(p, n):
    return (TOP - p - n, p)


def grp_a(p):
    return (TOP + p, TOP + p)


def own(j):
    return (4 * j, 4 * j)


def schedule(mid, eq):
    plan = {k: [] for k in range(NY + 1)}

    def put(k, kind, start, half=1):
        plan[k].append((kind, start[0] + 64 * start[1] + 4096 * half))

    first = 1 if eq else 10
    for j in range(10):
        put(first + j // 2, "big", own(j), 0)
    if mid and not eq:
        for i in range(3):
            put(4 * i + 4, "big", mine(4 * i, 4))
            put(4 * i + 5, "big", oth(4 * i, 4))
        put(6, "big", grp_a(0))
        put(10, "big", grp_a(4))
        put(12, "small", grp_a(8))
        put(15, "small", oth(12, 2))
        put(NY, "big", mine(12, 4))
    elif mid:
        order = [(9, 14, mine(0, 4)), (9, 14, oth(0, 4)), (10, 14, mine(4, 4)), (10, 14, oth(4, 4)), (11, 14, grp_a(0))]
        order += [(12, 15, mine(8, 4)), (13, 15, oth(8, 4)), (14, 15, grp_a(4))]
        for one, two, start in order:
            put(one, "part0", start)
            put(two, "part1", start)
        put(15, "small", oth(12, 2))
        put(15, "big", mine(12, 4))
        put(NY, "small", grp_a(8))
    elif not eq:
        put(3, "big", grp_a(0))
        put(7, "big", grp_a(4))
        put(9, "small", grp_a(8))
        put(6, "big", mine(0, 4))
        put(8, "small", mine(4, 2))
        put(13, "big", oth(10, 4))
        put(NY, "small", mine(14, 2))
    else:
        put(10, "big", grp_a(0))
        put(10, "big", grp_a(4))
        put(11, "small", grp_a(8))
        put(11, "big", mine(0, 4))
        put(12, "small", mine(4, 2))
        put(13, "big", oth(10, 4))
        put(NY, "small", mine(14, 2))
    return plan


def pick(key, table):
    code = jnp.int32(-1)
    for at, value in table:
        code = jnp.where(key == at, value, code)
    return code


def kernel(a_ref, b_ref, o_ref, am, bm, pm, ys, yr, zs, zr, as_, ar, bs, br, es, er, ps, pr, xs, xr, ds_, dr, fs, fr, ls, lr, loc):
    z, y, row = lax.axis_index("dep"), lax.axis_index("col"), lax.axis_index("row")
    x, c = row // 2, row % 2
    rows = a_ref.shape[0]
    quarter = b_ref.shape[0]
    width = o_ref.shape[1]
    ch = rows // PIECES
    kc = quarter // NK
    side = z // 2
    is_mid = (z == 1) | (z == 2)
    is_eq = x == y
    end_slice = 3 * side
    to_y = (z, 1 - y, row)
    to_x = (z, y, (1 - x) * 2 + c)
    to_core = (z, y, x * 2 + 1 - c)
    to_pair = (z + 1 - 2 * (z % 2), y, row)
    to_mid = (3 - z, y, row)

    def within(i, n):
        return jnp.clip(i, 0, n - 1)

    def span(start, n):
        return pl.ds(pl.multiple_of(start, n), n)

    def piece(p):
        return span(within(p, PIECES) * ch, ch)

    def mine_at(i):
        return i + side * (TOP - 1 - 2 * i)

    def oth_at(i):
        return TOP - 1 - i + side * (2 * i + 1 - TOP)

    def remote(src, dst, send, recv, dev):
        return pltpu.make_async_remote_copy(src_ref=src, dst_ref=dst, send_sem=send, recv_sem=recv, device_id=dev, device_id_type=MESH)

    def pass_rows(p, send, recv, dev):
        return remote(am.at[1, piece(p)], am.at[1, piece(p)], send, recv, dev)

    def copy_y(k, mid):
        p = mine_at(k) if mid else jnp.where(k < N_A, TOP + k, jnp.where(k < N_M, oth_at(k), mine_at(k)))
        k = within(k, NY)
        return remote(a_ref.at[piece(p)], am.at[1, piece(p)], ys.at[k], yr.at[k], to_y)

    def copy_zm(k):
        k = within(k, N_M)
        return pass_rows(mine_at(k), zs.at[k], zr.at[k], to_mid)

    def copy_ze(k):
        k = within(k, N_E)
        return pass_rows(mine_at(k), es.at[k], er.at[k], to_pair)

    def copy_za(k):
        k = within(k, N_A)
        return pass_rows(TOP + k, as_.at[k], ar.at[k], to_pair)

    def lane(i):
        return span(c * quarter + kc * i, kc)

    def copy_zb(i):
        i = within(i, NB)
        return remote(bm.at[1, lane(i)], bm.at[2, lane(i)], bs.at[i], br.at[i], to_pair)

    def b_piece(i, extra):
        early = i < extra
        return jnp.where(early, 2, 1), within(jnp.where(early, NB + i, i - extra), NK), early

    def copy_x(i, extra):
        slot, p, early = b_piece(i, extra)
        i = within(i, 2 * NK - NB)
        cols = pl.ds(pl.multiple_of(jnp.where(early, end_slice, z) * width, 128), width)
        return remote(b_ref.at[span(p * kc, kc), cols], bm.at[slot, lane(p)], xs.at[i], xr.at[i], to_x)

    def copy_d(i, extra):
        slot, p, _ = b_piece(i, extra)
        i = within(i, 2 * NK - NB)
        return remote(bm.at[slot, lane(p)], bm.at[slot, lane(p)], ds_.at[i], dr.at[i], to_core)

    def copy_f(i):
        i = within(i, NB)
        return remote(bm.at[2, lane(i)], bm.at[2, lane(i)], fs.at[i], fr.at[i], to_core)

    own_lane = span(c * quarter, quarter)

    def b_cols(s):
        return b_ref.at[:, pl.ds(pl.multiple_of(s * width, 128), width)]

    load_a = pltpu.make_async_copy(a_ref, am.at[0], loc.at[0])
    load_b = pltpu.make_async_copy(b_cols(z), bm.at[0, own_lane], loc.at[1])
    load_e = pltpu.make_async_copy(b_cols(end_slice), bm.at[2, own_lane], loc.at[2])
    give_b = remote(b_cols(z), bm.at[0, own_lane], ls.at[0], lr.at[0], to_core)
    give_e = remote(b_cols(end_slice), bm.at[2, own_lane], ls.at[1], lr.at[1], to_core)

    def sum_at(j):
        k, t = K_P + j // 2, j % 2
        last = k == K_P + 8
        from_oth = (t == 0) | last
        return jnp.where(from_oth, oth_at(jnp.where(last, 8 + t, k - K_P)), mine_at(k))

    def copy_p(j):
        j = within(j, N_P)
        ref = pm.at[span(j * ch, ch)]
        return remote(ref, ref, ps.at[j], pr.at[j], to_pair)

    barrier = pltpu.get_barrier_semaphore()
    for dev in (to_y, to_x, to_core, to_pair):
        pl.semaphore_signal(barrier, inc=1, device_id=dev, device_id_type=MESH)

    @pl.when(is_mid)
    def _():
        pl.semaphore_signal(barrier, inc=1, device_id=to_mid, device_id_type=MESH)

    load_b.start()
    load_a.start()
    pl.semaphore_wait(barrier, jnp.where(is_mid, 5, 4))

    def run(mid, eq):
        end = not mid
        sent_extra = NK - NB if mid and not eq else 0
        came_extra = NK - NB if mid and eq else 0
        n_send, n_recv = NK + sent_extra, NK + came_extra
        k_a = NB if eq else 0
        oth_slot, own_slot = (1, 0) if eq else (0, 1)
        plan = schedule(mid, eq)

        @pl.loop(0, NY)
        def _(k):
            copy_y(k, mid).start()

            @pl.when(k < n_send)
            def _():
                copy_x(k, sent_extra).start()

        give_b.start()
        if mid and not eq:
            load_e.start()
            give_e.start()

        @pl.loop(0, PIECES)
        def _(i):
            o_ref[span(i * ch, ch), :] = jnp.zeros((ch, width), jnp.float32)

        def multiply(kind, code):
            n = (2 if kind == "small" else 4) * ch
            half = code // 4096
            start = jnp.where(side == 0, code % 64, code // 64 % 64) * ch
            r = pl.ds(pl.multiple_of(jnp.clip(start, 0, rows - n), ch), n)
            if kind in ("big", "small"):
                slot = jnp.where(half == 1, oth_slot, own_slot)
                o_ref[r, :] += jnp.dot(am[half, r, :], bm[slot], preferred_element_type=jnp.float32)
                return
            lo, hi = (0, PART * kc) if kind == "part0" else (PART * kc, quarter)
            o_ref[r, :] += sum(
                jnp.dot(am[1, r, lo + q : hi + q], bm[1, lo + q : hi + q, :], preferred_element_type=jnp.float32)
                for q in (0, quarter)
            )

        def products(k, steps):
            for kind in ("big", "small", "part0", "part1"):
                by_step = {s: [v for name, v in plan[s] if name == kind] for s in steps}
                most = max(len(v) for v in by_step.values())
                if most == 0:
                    continue

                @pl.loop(0, most)
                def _(t):
                    code = pick(k * 8 + t, [(s * 8 + i, v) for s, vs in by_step.items() for i, v in enumerate(vs)])

                    @pl.when(code >= 0)
                    def _():
                        multiply(kind, code)

        def take_sums(j):
            j = within(j, N_P)
            copy_p(j).wait_recv()
            o_ref[piece(sum_at(j)), :] += pm[span(j * ch, ch), :]

        @pl.loop(0, NY)
        def _(k):
            copy_y(k, mid).wait_recv()

            if mid:

                @pl.when(k < N_M)
                def _():
                    copy_zm(k).start()

                @pl.when(k < N_E)
                def _():
                    copy_ze(k).start()

            @pl.when(k < n_recv)
            def _():
                copy_x(k, came_extra).wait_recv()
                copy_d(k, came_extra).start()

            if end:
                if eq:

                    @pl.when(k < NB)
                    def _():
                        copy_zb(k).start()

                @pl.when((k >= k_a) & (k < k_a + N_A))
                def _():
                    copy_za(k - k_a).start()

                @pl.when((k >= LAG) & (k < LAG + N_E))
                def _():
                    copy_ze(k - LAG).wait_recv()

            if mid:
                if eq:

                    @pl.when((k >= LAG) & (k < LAG + NB))
                    def _():
                        copy_zb(k - LAG).wait_recv()
                        copy_f(k - LAG).start()

                @pl.when((k >= LAG) & (k < LAG + N_M))
                def _():
                    copy_zm(k - LAG).wait_recv()

                @pl.when((k >= LAG + k_a) & (k < LAG + k_a + N_A))
                def _():
                    copy_za(k - LAG - k_a).wait_recv()

            @pl.when(k == 1)
            def _():
                load_b.wait()
                give_b.wait_recv()
                load_a.wait()
                if mid and not eq:
                    load_e.wait()
                    give_e.wait_recv()

            if mid:
                if eq:

                    @pl.when(k == K_P)
                    def _():
                        @pl.loop(0, NB)
                        def _(i):
                            copy_d(i, came_extra).wait_recv()
                            copy_f(i).wait_recv()

                @pl.when((k >= K_P) & (k < K_P + 9))
                def _():
                    @pl.loop(0, 2)
                    def _(t):
                        j = within(2 * (k - K_P) + t, N_P)
                        pm[span(j * ch, ch), :] = jnp.dot(am[1, piece(sum_at(j)), :], bm[2], preferred_element_type=jnp.float32)
                        copy_p(j).start()

            def b_ready(at, first, last):
                @pl.when(k == at)
                def _():
                    @pl.loop(first, last)
                    def _(i):
                        copy_d(i, came_extra).wait_recv()

            if mid and eq:
                b_ready(9, NB, NB + PART)
                b_ready(14, NB + PART, n_recv)
            else:
                b_ready(10, 0, NK)

            products(k, range(NY))

            if end:

                @pl.when(k >= K_P + 3)
                def _():
                    @pl.loop(0, 2)
                    def _(t):
                        take_sums(2 * (k - K_P - 3) + t)

        if mid and eq:

            @pl.loop(NY - LAG - k_a, N_A)
            def _(k):
                copy_za(k).wait_recv()

        products(jnp.int32(NY), [NY])

        if end:

            @pl.loop(2 * (NY - K_P - 3), N_P)
            def _(j):
                take_sums(j)

        @pl.loop(0, NY)
        def _(k):
            copy_y(k, mid).wait_send()

            @pl.when(k < n_send)
            def _():
                copy_x(k, sent_extra).wait_send()

            @pl.when(k < n_recv)
            def _():
                copy_d(k, came_extra).wait_send()

            if mid:

                @pl.when(k < N_M)
                def _():
                    copy_zm(k).wait_send()

                @pl.when(k < N_E)
                def _():
                    copy_ze(k).wait_send()

                if eq:

                    @pl.when(k < NB)
                    def _():
                        copy_f(k).wait_send()

            else:

                @pl.when(k < N_A)
                def _():
                    copy_za(k).wait_send()

                if eq:

                    @pl.when(k < NB)
                    def _():
                        copy_zb(k).wait_send()

        give_b.wait_send()
        if mid:
            if not eq:
                give_e.wait_send()

            @pl.loop(0, N_P)
            def _(j):
                copy_p(j).wait_send()

    for mid in (True, False):
        for eq in (True, False):

            @pl.when((is_mid == mid) & (is_eq == eq))
            def _():
                run(mid, eq)


def solution(mesh):
    def body(a, b):
        rows, depth = a.shape
        quarter, wide = b.shape
        width = wide // mesh.shape["dep"]
        dma = pltpu.SemaphoreType.DMA
        counts = (NY, NY, N_M, N_M, N_A, N_A, NB, NB, N_E, N_E, N_P, N_P, NY, NY, NY, NY, NB, NB, 2, 2, 3)
        return pl.pallas_call(
            kernel,
            out_shape=jax.ShapeDtypeStruct((rows, width), jnp.float32),
            in_specs=[pl.BlockSpec(memory_space=pl.ANY)] * 2,
            out_specs=pl.BlockSpec(memory_space=pltpu.VMEM),
            scratch_shapes=[
                pltpu.VMEM((2, rows, depth), jnp.bfloat16),
                pltpu.VMEM((3, 2 * quarter, width), jnp.bfloat16),
                pltpu.VMEM((N_P * (rows // PIECES), width), jnp.float32),
            ]
            + [dma((n,)) for n in counts],
            compiler_params=pltpu.CompilerParams(collective_id=0, has_side_effects=True, vmem_limit_bytes=48 * 2**20),
        )(a, b)

    return jax.shard_map(body, mesh=mesh, in_specs=(P("row", "col"), P("row", "col")), out_specs=P("row", ("col", "dep")), check_vma=False)
```

time: 359 us -> 70.2 us (0.20)
  waiting for transfers between devices: 316 us -> 0 us
  Pallas kernels: 0 us -> 68.4 us
  matrix products: 14.7 us -> 0 us
  local copies, waits for them, and re-layouts: 14.9 us -> 1.71 us
  between operations: 13.1 us -> 0.01 us
    reduce_scatter x1 -> x0, waiting for transfers between devices: 220 us -> none  [local_product(): return lax.psum_scatter(part_sum, 'dep', scatter_dimension=1, tiled=True)]
    all_gather x2 -> x0, waiting for transfers between devices: 96 us -> none  [the longest x1 49.5 us: local_product(): b_panel = lax.all_gather(b_part, 'row', axis=0, tiled=True)]
    pallas_call x0 -> x1, Pallas kernels: none -> 68.4 us  [body(): pl.pallas_call(kernel, out_shape=jax.ShapeDtypeStruct((rows, width), jnp....]
    dot_general x1 -> x0, matrix products: 14.7 us -> none  [local_product(): part_sum = jnp.dot(a_panel, b_panel, preferred_element_type=jnp.float32)]
    unnamed x1, local copies, waits for them, and re-layouts: 9.5 us -> 1.71 us
    dynamic_slice x2 -> x0, local copies, waits for them, and re-layouts: 5.42 us -> none  [the longest x1 2.72 us: local_product(): b_part = lax.dynamic_index_in_dim(b_part, layer_idx, axis=1, keepdims=False)]
  transfers between devices with their start and end apart: 3 -> 0, of which waited for: 3 -> 0; matrix products, arithmetic and copies ran while one was open for 1% -> 0% of each run, Pallas kernels for 0% -> 0%
where the time goes in v2:
time: 70.2 us; the launch traced here: 70.1 us
  Pallas kernels  68.4 us (97%)
  local copies, waits for them, and re-layouts  1.71 us (2%)
    pallas_call x1, Pallas kernels, body(): pl.pallas_call(kernel, out_shape=jax.ShapeDtypeStruct((rows, width), jnp....  68.4 us
    unnamed x1, local copies, waits for them, and re-layouts  1.71 us

profile of v2, /device:TPU:0, one launch (start us, length us, event | category | flops | bytes accessed | tf_op | source)
XLA Modules:
  0.0 70.1 jit_solution(11160435752599351694)
XLA Ops:
  0.0 68.4 %shard_map.28 = f32[1280,640]{1,0:T(8,128)S(1)} custom-call(bf16[1280,2560]{1,0:T(8,128)(2,1)} %a_ref.1, bf16[1280,2560]{1,0:T(8,128)(2,1)} %b_ref.1), custom_call_target="tpu_custom_call" | custom-call | tf_op jit(solution)/shard_map/pallas_call | solution.py:448
  68.4 1.7 %copy.4 = f32[1280,640]{1,0:T(8,128)} copy(f32[1280,640]{1,0:T(8,128)S(1)} %shard_map.28) | data formatting | bytes 6553600

commit v3 on v2

v3 whole, which is shorter than its diff:
```python
import jax
import jax.numpy as jnp
from jax import lax
from jax.experimental import pallas as pl
from jax.experimental.pallas import tpu as pltpu
from jax.sharding import PartitionSpec as P

MESH = pl.DeviceIdType.MESH

PIECES = 40
NY = 16
N_A = 10
N_M = 14
TOP = 30
N_E = 5
NK = 10
NB = 4
N_X = NK - NB
K_P = 5
N_P = 19
LAG = 2
PART = 6
ROWS = {"big": 4, "small": 2, "tiny": 1, "part0": 4, "part1": 8, "part1w": 12}


def mine(p, n):
    return (p, TOP - p - n)


def oth(p, n):
    return (TOP - p - n, p)


def grp_a(p):
    return (TOP + p, TOP + p)


def own(j):
    return (4 * j, 4 * j)


def schedule(mid, eq):
    plan = {k: [] for k in range(NY + 1)}

    def put(k, kind, start, half=1):
        plan[k].append((kind, start[0] + 64 * start[1] + 4096 * half))

    first = 1 if eq else 10
    for j in range(10):
        put(first + j // 2, "big", own(j), 0)
    if mid and not eq:
        for i in range(3):
            put(4 * i + 4, "big", mine(4 * i, 4))
            put(4 * i + 5, "big", oth(4 * i, 4))
        put(6, "big", grp_a(0))
        put(9, "big", grp_a(4))
        put(15, "small", grp_a(8))
    elif mid:
        order = [(12, mine(0, 4)), (12, oth(0, 4)), (12, grp_a(0)), (13, mine(4, 4)), (13, oth(4, 4)), (13, mine(8, 4))]
        order += [(14, oth(8, 4)), (14, grp_a(4))]
        for k, start in order:
            put(k, "part0", start)
        put(14, "part1w", mine(0, 12))
        put(14, "part1w", oth(0, 12))
        put(14, "part1", grp_a(0))
    else:
        late = eq
        put(10 if late else 3, "big", grp_a(0))
        put(10 if late else 7, "big", grp_a(4))
        put(11 if late else 9, "small", grp_a(8))
        put(11 if late else 6, "big", mine(0, 4))
        put(12 if late else 8, "tiny", mine(4, 1))
        put(13, "big", oth(10, 4))
        put(NY, "small", mine(14, 2))
    return plan


def pick(key, table):
    code = jnp.int32(-1)
    for at, value in table:
        code = jnp.where(key == at, value, code)
    return code


def kernel(a_ref, b_ref, o_ref, am, bm, pm, yr, gr, hr, br, xr, dr, lr, sent):
    z, y, row = lax.axis_index("dep"), lax.axis_index("col"), lax.axis_index("row")
    x, c = row // 2, row % 2
    rows = a_ref.shape[0]
    quarter = b_ref.shape[0]
    width = o_ref.shape[1]
    ch = rows // PIECES
    kc = quarter // NK
    side = z // 2
    is_mid = (z == 1) | (z == 2)
    is_eq = x == y
    pair = z + 1 - 2 * (z % 2)
    to_y = (z, 1 - y, row)
    to_x = (z, y, (1 - x) * 2 + c)
    to_core = (z, y, x * 2 + 1 - c)
    to_pair = (pair, y, row)
    to_mid = (3 - z, y, row)

    def within(i, n):
        return jnp.clip(i, 0, n - 1)

    def span(start, n):
        return pl.ds(pl.multiple_of(start, n), n)

    def piece(p):
        return span(within(p, PIECES) * ch, ch)

    def mine_at(i):
        return i + side * (TOP - 1 - 2 * i)

    def oth_at(i):
        return TOP - 1 - i + side * (2 * i + 1 - TOP)

    def remote(src, dst, send, recv, dev):
        return pltpu.make_async_remote_copy(src_ref=src, dst_ref=dst, send_sem=send, recv_sem=recv, device_id=dev, device_id_type=MESH)

    def pass_rows(p, flow, recv, dev):
        return remote(am.at[1, piece(p)], am.at[1, piece(p)], sent.at[flow], recv, dev)

    def copy_y(k, mid):
        p = mine_at(k) if mid else jnp.where(k < N_A, TOP + k, jnp.where(k < N_M, oth_at(k), mine_at(k)))
        return remote(a_ref.at[piece(p)], am.at[1, piece(p)], sent.at[0], yr.at[within(k, NY)], to_y)

    def copy_zm(k):
        k = within(k, N_M)
        return pass_rows(mine_at(k), 1, gr.at[k], to_mid)

    def copy_ze(k):
        k = within(k, N_E)
        return pass_rows(mine_at(k), 2, hr.at[k], to_pair)

    def copy_za(k):
        k = within(k, N_A)
        return pass_rows(TOP + k, 1, hr.at[k], to_pair)

    def lane(i, n=1, core=c):
        return pl.ds(pl.multiple_of(core * quarter + kc * i, kc), n * kc)

    def copy_zb(i):
        i = within(i, NB)
        return remote(bm.at[1, lane(i)], bm.at[2, lane(i)], sent.at[2], br.at[i], to_pair)

    copy_zc = remote(bm.at[2, lane(NK - 1)], bm.at[1, lane(NK - 1)], sent.at[2], br.at[NB], to_pair)

    def b_piece(i, mid, special):
        if not special:
            return 1, within(i, NK), z
        extra = (i < N_X) if mid else (i == NK)
        other = within(NB + i, NK) if mid else NK - 1
        plain = within(i - N_X if mid else i, NK)
        return jnp.where(extra, 2, 1), jnp.where(extra, other, plain), jnp.where(extra, pair, z)

    def copy_x(i, mid, special):
        slot, p, s = b_piece(i, mid, special)
        cols = pl.ds(pl.multiple_of(s * width, 128), width)
        rows_b = pl.ds(pl.multiple_of(p * kc, kc), kc)
        return remote(b_ref.at[rows_b, cols], bm.at[slot, lane(p)], sent.at[3], xr.at[within(i, NY)], to_x)

    def copy_d(slot, p, group):
        return remote(bm.at[slot, lane(p)], bm.at[slot, lane(p)], sent.at[4], dr.at[group], to_core)

    def came_d(slot, p, n, group):
        ref = bm.at[slot, lane(p, n, 1 - c)]
        remote(ref, ref, sent.at[4], dr.at[group], to_core).wait_recv()

    def all_sent(flow, ref):
        remote(ref, ref, sent.at[flow], lr.at[0], to_core).wait_send()

    own_lane = span(c * quarter, quarter)

    def b_cols(s):
        return b_ref.at[:, pl.ds(pl.multiple_of(s * width, 128), width)]

    load_a = pltpu.make_async_copy(a_ref, am.at[0], lr.at[2])
    load_b = pltpu.make_async_copy(b_cols(z), bm.at[0, own_lane], lr.at[3])
    load_e = pltpu.make_async_copy(b_cols(pair), bm.at[2, own_lane], lr.at[4])
    give_b = remote(b_cols(z), bm.at[0, own_lane], sent.at[5], lr.at[0], to_core)
    give_e = remote(b_cols(pair), bm.at[2, own_lane], sent.at[6], lr.at[1], to_core)

    def sum_at(j):
        k = K_P + j // 2
        return jnp.where(j % 2 == 0, oth_at(k - K_P), mine_at(k))

    def copy_p(j):
        j = within(j, N_P)
        ref = pm.at[span(j * ch, ch)]
        return remote(ref, ref, sent.at[7], gr.at[j // 2], to_pair)

    def came_p(j, n):
        ref = pm.at[pl.ds(pl.multiple_of(within(j, N_P - n + 1) * ch, ch), n * ch)]
        remote(ref, ref, sent.at[7], gr.at[within(j // 2, (N_P + 1) // 2)], to_pair).wait_recv()

    barrier = pltpu.get_barrier_semaphore()
    for dev in (to_y, to_x, to_core, to_pair):
        pl.semaphore_signal(barrier, inc=1, device_id=dev, device_id_type=MESH)

    @pl.when(is_mid)
    def _():
        pl.semaphore_signal(barrier, inc=1, device_id=to_mid, device_id_type=MESH)

    load_b.start()
    load_a.start()
    pl.semaphore_wait(barrier, jnp.where(is_mid, 5, 4))

    def run(mid, eq):
        end = not mid
        extra = N_X - 1 if mid else 1
        n_send, n_recv = (NK, NK + extra) if eq else (NK + extra, NK)
        k_a, wait_a = (NB, NB + LAG + 1) if eq else (0, LAG)
        oth_slot, own_slot = (1, 0) if eq else (0, 1)
        plan = schedule(mid, eq)

        @pl.loop(0, NY)
        def _(k):
            copy_y(k, mid).start()

            @pl.when(k < n_send)
            def _():
                copy_x(k, mid, not eq).start()

        give_b.start()
        if mid and not eq:
            load_e.start()
            give_e.start()

        @pl.loop(0, PIECES)
        def _(i):
            o_ref[span(i * ch, ch), :] = jnp.zeros((ch, width), jnp.float32)

        def multiply(kind, code):
            n = ROWS[kind] * ch
            half = code // 4096
            start = jnp.where(side == 0, code % 64, code // 64 % 64) * ch
            r = pl.ds(pl.multiple_of(jnp.clip(start, 0, rows - n), ch), n)
            if kind in ("big", "small", "tiny"):
                slot = jnp.where(half == 1, oth_slot, own_slot)
                o_ref[r, :] += jnp.dot(am[half, r, :], bm[slot], preferred_element_type=jnp.float32)
                return
            lo, hi = (0, PART * kc) if kind == "part0" else (PART * kc, quarter)
            o_ref[r, :] += sum(
                jnp.dot(am[1, r, lo + q : hi + q], bm[1, lo + q : hi + q, :], preferred_element_type=jnp.float32)
                for q in (0, quarter)
            )

        def products(k, steps):
            for kind in ROWS:
                by_step = {s: [v for name, v in plan[s] if name == kind] for s in steps}
                most = max(len(v) for v in by_step.values())
                if most == 0:
                    continue

                @pl.loop(0, most)
                def _(t):
                    code = pick(k * 8 + t, [(s * 8 + i, v) for s, vs in by_step.items() for i, v in enumerate(vs)])

                    @pl.when(code >= 0)
                    def _():
                        multiply(kind, code)

        def take_sums(j):
            j = within(j, N_P)
            o_ref[piece(sum_at(j)), :] += pm[span(j * ch, ch), :]

        @pl.loop(0, NY)
        def _(k):
            copy_y(k, mid).wait_recv()

            if mid:

                @pl.when(k < N_M)
                def _():
                    copy_zm(k).start()

                @pl.when(k < N_E)
                def _():
                    copy_ze(k).start()

            @pl.when(k < n_recv)
            def _():
                copy_x(k, mid, eq).wait_recv()

            @pl.when(k < (NK if end else n_recv))
            def _():
                slot, p, _ = b_piece(k, mid, eq and mid)
                group = 0
                if mid and eq:
                    group = jnp.where(k < N_X, 0, jnp.where(k < N_X + PART, 1, 2))
                copy_d(slot, p, group).start()

            if end:
                if eq:

                    @pl.when(k < NB)
                    def _():
                        copy_zb(k).start()

                    @pl.when(k == NK)
                    def _():
                        copy_zc.start()

                @pl.when((k >= k_a) & (k < k_a + N_A))
                def _():
                    copy_za(k - k_a).start()

                @pl.when((k >= LAG) & (k < LAG + N_E))
                def _():
                    copy_ze(k - LAG).wait_recv()

            if mid:
                if eq:

                    @pl.when((k >= LAG) & (k < LAG + NB))
                    def _():
                        copy_zb(k - LAG).wait_recv()
                        copy_d(2, within(k - LAG, NB), 3).start()

                    @pl.when(k == 13)
                    def _():
                        copy_zc.wait_recv()
                        copy_d(1, NK - 1, 2).start()

                @pl.when((k >= LAG) & (k < LAG + N_M))
                def _():
                    copy_zm(k - LAG).wait_recv()

                @pl.when((k >= wait_a) & (k < wait_a + N_A))
                def _():
                    copy_za(k - wait_a).wait_recv()

            @pl.when(k == 1)
            def _():
                load_b.wait()
                give_b.wait_recv()
                load_a.wait()
                if mid and not eq:
                    load_e.wait()
                    give_e.wait_recv()

            if mid:
                if eq:

                    @pl.when(k == K_P)
                    def _():
                        came_d(2, NB, N_X, 0)
                        came_d(2, 0, NB, 3)

                @pl.when((k >= K_P) & (k < K_P + (N_P + 1) // 2))
                def _():
                    @pl.loop(2 * (k - K_P), jnp.minimum(2 * (k - K_P) + 2, N_P))
                    def _(j):
                        pm[span(j * ch, ch), :] = jnp.dot(am[1, piece(sum_at(j)), :], bm[2], preferred_element_type=jnp.float32)
                        copy_p(j).start()

            if mid and eq:

                @pl.when(k == 12)
                def _():
                    came_d(1, 0, PART, 1)

                @pl.when(k == 14)
                def _():
                    came_d(1, PART, NK - PART, 2)

            else:

                @pl.when(k == 10)
                def _():
                    came_d(1, 0, NK, 0)

            products(k, range(NY))

            if end:

                @pl.when(k >= K_P + 3)
                def _():
                    came_p(2 * (k - K_P - 3), 2)

                    @pl.loop(0, 2)
                    def _(t):
                        take_sums(2 * (k - K_P - 3) + t)

        if mid and eq:

            @pl.loop(NY - wait_a, N_A)
            def _(k):
                copy_za(k).wait_recv()

        if mid:
            last = [(mine(12, 4), 4), (oth(12, 2), 2)] + ([(grp_a(8), 2)] if eq else [])
            spans = [pl.ds(pl.multiple_of((s0 + side * (s1 - s0)) * ch, ch), n * ch) for (s0, s1), n in last]
            left = jnp.concatenate([am[1, r, :] for r in spans], axis=0)
            total = jnp.dot(left, bm[oth_slot], preferred_element_type=jnp.float32)
            at = 0
            for r, (_, n) in zip(spans, last):
                o_ref[r, :] += total[at : at + n * ch]
                at += n * ch
        else:
            products(jnp.int32(NY), [NY])

            @pl.loop(2 * (NY - K_P - 3), N_P, step=2)
            def _(j):
                @pl.when(j < N_P - 1)
                def _():
                    came_p(j, 2)
                    take_sums(j)
                    take_sums(j + 1)

            came_p(N_P - 1, 1)
            take_sums(N_P - 1)

        all_sent(0, am.at[0, pl.ds(0, NY * ch)])
        all_sent(1, am.at[0, pl.ds(0, (N_M if mid else N_A) * ch)])
        if mid:
            all_sent(2, am.at[0, pl.ds(0, N_E * ch)])
            all_sent(7, pm)
        elif eq:
            all_sent(2, bm.at[0, pl.ds(0, (NB + 1) * kc)])
        all_sent(3, bm.at[0, pl.ds(0, n_send * kc)])
        all_sent(4, bm.at[0, pl.ds(0, (2 * NK if mid and eq else NK) * kc)])
        all_sent(5, bm.at[0, pl.ds(0, quarter)])
        if mid and not eq:
            all_sent(6, bm.at[0, pl.ds(0, quarter)])

    for mid in (True, False):
        for eq in (True, False):

            @pl.when((is_mid == mid) & (is_eq == eq))
            def _():
                run(mid, eq)


def solution(mesh):
    def body(a, b):
        rows, depth = a.shape
        quarter, wide = b.shape
        width = wide // mesh.shape["dep"]
        dma = pltpu.SemaphoreType.DMA
        counts = (NY, N_M, N_A, NB + 1, NY, 4, 5, 8)
        return pl.pallas_call(
            kernel,
            out_shape=jax.ShapeDtypeStruct((rows, width), jnp.float32),
            in_specs=[pl.BlockSpec(memory_space=pl.ANY)] * 2,
            out_specs=pl.BlockSpec(memory_space=pltpu.VMEM),
            scratch_shapes=[
                pltpu.VMEM((2, rows, depth), jnp.bfloat16),
                pltpu.VMEM((3, 2 * quarter, width), jnp.bfloat16),
                pltpu.VMEM((N_P * (rows // PIECES), width), jnp.float32),
            ]
            + [dma((n,)) for n in counts],
            compiler_params=pltpu.CompilerParams(collective_id=0, has_side_effects=True, vmem_limit_bytes=48 * 2**20),
        )(a, b)

    return jax.shard_map(body, mesh=mesh, in_specs=(P("row", "col"), P("row", "col")), out_specs=P("row", ("col", "dep")), check_vma=False)
```

time: 70.2 us -> 66.9 us (0.953)
  Pallas kernels: 68.4 us -> 65.1 us
    pallas_call x1, Pallas kernels: 68.4 us -> 65.1 us  [body(): pl.pallas_call(kernel, out_shape=jax.ShapeDtypeStruct((rows, width), jnp....]
where the time goes in v3:
time: 66.9 us; the launch traced here: 66.8 us
  Pallas kernels  65.1 us (97%)
  local copies, waits for them, and re-layouts  1.71 us (3%)
    pallas_call x1, Pallas kernels, body(): pl.pallas_call(kernel, out_shape=jax.ShapeDtypeStruct((rows, width), jnp....  65.1 us
    unnamed x1, local copies, waits for them, and re-layouts  1.71 us

profile of v3, /device:TPU:0, one launch (start us, length us, event | category | flops | bytes accessed | tf_op | source)
XLA Modules:
  0.0 66.8 jit_solution(3979042451192071515)
XLA Ops:
  0.0 65.1 %shard_map.28 = f32[1280,640]{1,0:T(8,128)S(1)} custom-call(bf16[1280,2560]{1,0:T(8,128)(2,1)} %a_ref.1, bf16[1280,2560]{1,0:T(8,128)(2,1)} %b_ref.1), custom_call_target="tpu_custom_call" | custom-call | tf_op jit(solution)/shard_map/pallas_call | solution.py:443
  65.1 1.7 %copy.4 = f32[1280,640]{1,0:T(8,128)} copy(f32[1280,640]{1,0:T(8,128)S(1)} %shard_map.28) | data formatting | bytes 6553600

commit v4 on v3

--- a/solution.py
+++ b/solution.py
@@ -19,8 +19,18 @@
 K_P = 5
 N_P = 19
 LAG = 2
-PART = 6
-ROWS = {"big": 4, "small": 2, "tiny": 1, "part0": 4, "part1": 8, "part1w": 12}
+PARTS = (0, 6, 8, NK)
+KINDS = {
+    "big": (4, None),
+    "small": (2, None),
+    "tiny": (1, None),
+    "first4": (4, 0),
+    "first12": (12, 0),
+    "next8": (8, 1),
+    "next12": (12, 1),
+    "rest8": (8, 2),
+    "rest12": (12, 2),
+}
 
 
 def mine(p, n):
@@ -42,8 +52,8 @@
 def schedule(mid, eq):
     plan = {k: [] for k in range(NY + 1)}
 
-    def put(k, kind, start, half=1):
-        plan[k].append((kind, start[0] + 64 * start[1] + 4096 * half))
+    def put(k, kind, start, half=1, late=0, only=False):
+        plan[k].append((kind, start[0] + 64 * start[1] + 4096 * half, late, only))
 
     first = 1 if eq else 10
     for j in range(10):
@@ -51,18 +61,19 @@
     if mid and not eq:
         for i in range(3):
             put(4 * i + 4, "big", mine(4 * i, 4))
-            put(4 * i + 5, "big", oth(4 * i, 4))
+            put(4 * i + 5, "big", oth(4 * i, 4), late=1)
         put(6, "big", grp_a(0))
         put(9, "big", grp_a(4))
         put(15, "small", grp_a(8))
     elif mid:
-        order = [(12, mine(0, 4)), (12, oth(0, 4)), (12, grp_a(0)), (13, mine(4, 4)), (13, oth(4, 4)), (13, mine(8, 4))]
-        order += [(14, oth(8, 4)), (14, grp_a(4))]
-        for k, start in order:
-            put(k, "part0", start)
-        put(14, "part1w", mine(0, 12))
-        put(14, "part1w", oth(0, 12))
-        put(14, "part1", grp_a(0))
+        put(12, "first12", mine(0, 12))
+        put(12, "first4", grp_a(0))
+        put(13, "first12", oth(0, 12), late=1)
+        put(14, "first4", grp_a(4))
+        for part in ("next", "rest"):
+            put(14, part + "12", mine(0, 12))
+            put(14, part + "12", oth(0, 12))
+            put(14, part + "8", grp_a(0))
     else:
         late = eq
         put(10 if late else 3, "big", grp_a(0))
@@ -70,6 +81,7 @@
         put(11 if late else 9, "small", grp_a(8))
         put(11 if late else 6, "big", mine(0, 4))
         put(12 if late else 8, "tiny", mine(4, 1))
+        put(12 if late else 8, "tiny", mine(5, 1), only=True)
         put(13, "big", oth(10, 4))
         put(NY, "small", mine(14, 2))
     return plan
@@ -94,6 +106,7 @@
     is_mid = (z == 1) | (z == 2)
     is_eq = x == y
     pair = z + 1 - 2 * (z % 2)
+    n_e, n_p, k_p = N_E + c, N_P - c, K_P + c
     to_y = (z, 1 - y, row)
     to_x = (z, y, (1 - x) * 2 + c)
     to_core = (z, y, x * 2 + 1 - c)
@@ -130,7 +143,7 @@
         return pass_rows(mine_at(k), 1, gr.at[k], to_mid)
 
     def copy_ze(k):
-        k = within(k, N_E)
+        k = within(k, N_E + 1)
         return pass_rows(mine_at(k), 2, hr.at[k], to_pair)
 
     def copy_za(k):
@@ -182,8 +195,8 @@
     give_e = remote(b_cols(pair), bm.at[2, own_lane], sent.at[6], lr.at[1], to_core)
 
     def sum_at(j):
-        k = K_P + j // 2
-        return jnp.where(j % 2 == 0, oth_at(k - K_P), mine_at(k))
+        k = j // 2 + k_p - 1
+        return jnp.where(j < 3, oth_at(j), jnp.where(j == 3, mine_at(k_p), jnp.where(j % 2 == 0, mine_at(k), oth_at(k - 3 - c))))
 
     def copy_p(j):
         j = within(j, N_P)
@@ -232,30 +245,43 @@
             o_ref[span(i * ch, ch), :] = jnp.zeros((ch, width), jnp.float32)
 
         def multiply(kind, code):
-            n = ROWS[kind] * ch
+            n, part = KINDS[kind]
+            n = n * ch
             half = code // 4096
             start = jnp.where(side == 0, code % 64, code // 64 % 64) * ch
             r = pl.ds(pl.multiple_of(jnp.clip(start, 0, rows - n), ch), n)
-            if kind in ("big", "small", "tiny"):
+            if part is None:
                 slot = jnp.where(half == 1, oth_slot, own_slot)
                 o_ref[r, :] += jnp.dot(am[half, r, :], bm[slot], preferred_element_type=jnp.float32)
                 return
-            lo, hi = (0, PART * kc) if kind == "part0" else (PART * kc, quarter)
+            lo, hi = PARTS[part] * kc, PARTS[part + 1] * kc
             o_ref[r, :] += sum(
                 jnp.dot(am[1, r, lo + q : hi + q], bm[1, lo + q : hi + q, :], preferred_element_type=jnp.float32)
                 for q in (0, quarter)
             )
 
         def products(k, steps):
-            for kind in ROWS:
-                by_step = {s: [v for name, v in plan[s] if name == kind] for s in steps}
-                most = max(len(v) for v in by_step.values())
+            for kind in KINDS:
+                if mid and eq and kind in ("next8", "rest8"):
+                    part = KINDS[kind][1]
+
+                    @pl.when(k == 14)
+                    def _():
+                        came_d(1, PARTS[part], PARTS[part + 1] - PARTS[part], 1 + part)
+
+                table, most = {}, 0
+                for core in (0, 1):
+                    for step in steps:
+                        found = [e for s in plan for e in plan[s] if e[0] == kind and s + core * e[2] == step and core >= e[3]]
+                        most = max(most, len(found))
+                        for i, e in enumerate(found):
+                            table.setdefault(e, [-1, -1])[core] = step * 8 + i
                 if most == 0:
                     continue
 
                 @pl.loop(0, most)
                 def _(t):
-                    code = pick(k * 8 + t, [(s * 8 + i, v) for s, vs in by_step.items() for i, v in enumerate(vs)])
+                    code = pick(k * 8 + t, [(jnp.where(c == 1, one, zero), e[1]) for e, (zero, one) in table.items()])
 
                     @pl.when(code >= 0)
                     def _():
@@ -275,7 +301,7 @@
                 def _():
                     copy_zm(k).start()
 
-                @pl.when(k < N_E)
+                @pl.when(k < n_e)
                 def _():
                     copy_ze(k).start()
 
@@ -288,7 +314,7 @@
                 slot, p, _ = b_piece(k, mid, eq and mid)
                 group = 0
                 if mid and eq:
-                    group = jnp.where(k < N_X, 0, jnp.where(k < N_X + PART, 1, 2))
+                    group = jnp.where(k < N_X, 0, jnp.where(k < N_X + PARTS[1], 1, jnp.where(k < N_X + PARTS[2], 2, 3)))
                 copy_d(slot, p, group).start()
 
             if end:
@@ -306,7 +332,7 @@
                 def _():
                     copy_za(k - k_a).start()
 
-                @pl.when((k >= LAG) & (k < LAG + N_E))
+                @pl.when((k >= LAG) & (k < LAG + n_e))
                 def _():
                     copy_ze(k - LAG).wait_recv()
 
@@ -316,20 +342,12 @@
                     @pl.when((k >= LAG) & (k < LAG + NB))
                     def _():
                         copy_zb(k - LAG).wait_recv()
-                        copy_d(2, within(k - LAG, NB), 3).start()
+                        copy_d(2, within(k - LAG, NB), 4).start()
 
                     @pl.when(k == 13)
                     def _():
                         copy_zc.wait_recv()
-                        copy_d(1, NK - 1, 2).start()
-
-                @pl.when((k >= LAG) & (k < LAG + N_M))
-                def _():
-                    copy_zm(k - LAG).wait_recv()
-
-                @pl.when((k >= wait_a) & (k < wait_a + N_A))
-                def _():
-                    copy_za(k - wait_a).wait_recv()
+                        copy_d(1, NK - 1, 3).start()
 
             @pl.when(k == 1)
             def _():
@@ -343,27 +361,35 @@
             if mid:
                 if eq:
 
-                    @pl.when(k == K_P)
+                    @pl.when(k == k_p)
                     def _():
                         came_d(2, NB, N_X, 0)
-                        came_d(2, 0, NB, 3)
-
-                @pl.when((k >= K_P) & (k < K_P + (N_P + 1) // 2))
-                def _():
-                    @pl.loop(2 * (k - K_P), jnp.minimum(2 * (k - K_P) + 2, N_P))
+                        came_d(2, 0, NB, 4)
+
+                @pl.when((k >= k_p) & (k < k_p + N_P // 2))
+                def _():
+                    j0 = jnp.where(k == k_p, 0, 2 * (k - k_p) + 2)
+
+                    @pl.loop(j0, jnp.minimum(2 * (k - k_p) + 4, n_p))
                     def _(j):
                         pm[span(j * ch, ch), :] = jnp.dot(am[1, piece(sum_at(j)), :], bm[2], preferred_element_type=jnp.float32)
                         copy_p(j).start()
 
+            if mid:
+
+                @pl.when((k >= LAG + c) & (k < LAG + c + N_M))
+                def _():
+                    copy_zm(k - LAG - c).wait_recv()
+
+                @pl.when((k >= wait_a) & (k < wait_a + N_A))
+                def _():
+                    copy_za(k - wait_a).wait_recv()
+
             if mid and eq:
 
                 @pl.when(k == 12)
                 def _():
-                    came_d(1, 0, PART, 1)
-
-                @pl.when(k == 14)
-                def _():
-                    came_d(1, PART, NK - PART, 2)
+                    came_d(1, 0, PARTS[1], 1)
 
             else:
 
@@ -390,6 +416,11 @@
                 copy_za(k).wait_recv()
 
         if mid:
+
+            @pl.when(c == 1)
+            def _():
+                copy_zm(N_M - 1).wait_recv()
+
             last = [(mine(12, 4), 4), (oth(12, 2), 2)] + ([(grp_a(8), 2)] if eq else [])
             spans = [pl.ds(pl.multiple_of((s0 + side * (s1 - s0)) * ch, ch), n * ch) for (s0, s1), n in last]
             left = jnp.concatenate([am[1, r, :] for r in spans], axis=0)
@@ -409,14 +440,26 @@
                     take_sums(j)
                     take_sums(j + 1)
 
-            came_p(N_P - 1, 1)
-            take_sums(N_P - 1)
+            @pl.when(c == 0)
+            def _():
+                came_p(N_P - 1, 1)
+                take_sums(N_P - 1)
+
 
         all_sent(0, am.at[0, pl.ds(0, NY * ch)])
         all_sent(1, am.at[0, pl.ds(0, (N_M if mid else N_A) * ch)])
         if mid:
-            all_sent(2, am.at[0, pl.ds(0, N_E * ch)])
-            all_sent(7, pm)
+
+            @pl.when(c == 0)
+            def _():
+                all_sent(2, am.at[0, pl.ds(0, N_E * ch)])
+                all_sent(7, pm)
+
+            @pl.when(c == 1)
+            def _():
+                all_sent(2, am.at[0, pl.ds(0, (N_E + 1) * ch)])
+                all_sent(7, pm.at[pl.ds(0, (N_P - 1) * ch)])
+
         elif eq:
             all_sent(2, bm.at[0, pl.ds(0, (NB + 1) * kc)])
         all_sent(3, bm.at[0, pl.ds(0, n_send * kc)])
@@ -439,7 +482,7 @@
         quarter, wide = b.shape
         width = wide // mesh.shape["dep"]
         dma = pltpu.SemaphoreType.DMA
-        counts = (NY, N_M, N_A, NB + 1, NY, 4, 5, 8)
+        counts = (NY, N_M, N_A, NB + 1, NY, 5, 5, 8)
         return pl.pallas_call(
             kernel,
             out_shape=jax.ShapeDtypeStruct((rows, width), jnp.float32),

time: 66.9 us -> 66 us (0.987)
  Pallas kernels: 65.1 us -> 64.1 us
    pallas_call x1, Pallas kernels: 65.1 us -> 64.1 us  [body(): pl.pallas_call(kernel, out_shape=jax.ShapeDtypeStruct((rows, width), jnp....]
where the time goes in v4:
time: 66 us; the launch traced here: 65.8 us
  Pallas kernels  64.1 us (97%)
  local copies, waits for them, and re-layouts  1.71 us (3%)
    pallas_call x1, Pallas kernels, body(): pl.pallas_call(kernel, out_shape=jax.ShapeDtypeStruct((rows, width), jnp....  64.1 us
    unnamed x1, local copies, waits for them, and re-layouts  1.71 us

profile of v4, /device:TPU:0, one launch (start us, length us, event | category | flops | bytes accessed | tf_op | source)
XLA Modules:
  0.0 65.8 jit_solution(6001437886761721288)
XLA Ops:
  0.0 64.1 %shard_map.28 = f32[1280,640]{1,0:T(8,128)S(1)} custom-call(bf16[1280,2560]{1,0:T(8,128)(2,1)} %a_ref.1, bf16[1280,2560]{1,0:T(8,128)(2,1)} %b_ref.1), custom_call_target="tpu_custom_call" | custom-call | tf_op jit(solution)/shard_map/pallas_call | solution.py:486
  64.1 1.7 %copy.4 = f32[1280,640]{1,0:T(8,128)} copy(f32[1280,640]{1,0:T(8,128)S(1)} %shard_map.28) | data formatting | bytes 6553600
